TPU v7x, 32 devices: a whole 2x2x4 slice. The times are simulated.
32 devices in a mesh: groups: 2 (over x), tm: 4 (over y, core), rows: 4 (over z).
Axes of the slice: x: 2, y: 2, z: 4, core: 2. Of those that a mesh axis runs over, the one named last changes fastest.
Arguments:
- features: bfloat16 [16, 8, 96, 512], P(('groups', 'tm'), 'rows'), parts along dimension 0, may hold values from -6 to 6
- spatial_weight: bfloat16 [3, 3, 512, 512], replicated, may hold values from -0.09375 to 0.09375
- temporal_weight: bfloat16 [3, 512, 512], replicated, may hold values from -0.15625 to 0.15625
- head_weight: bfloat16 [512, 16], replicated, may hold values from -0.25 to 0.25
- embed_weight: bfloat16 [64, 5120], replicated, may hold values from -0.75 to 0.75
- ada_scale: bfloat16 [5120], replicated, may hold values from -0.5 to 0.5
- ada_shift: bfloat16 [5120], replicated, may hold values from -3 to 3
- qkv_weight: bfloat16 [5120, 9216], P('tm', 'rows'), may hold values from -0.078125 to 0.078125
Outputs:
- qkv: float32 [3072, 9216], P(('groups', 'tm'), 'rows'), parts along dimension 0
There are 2 independent parts, one for each index of `groups`. A program takes and returns all parts, laid end to end along the dimension named above; an argument that names none is the same for every part. Nothing has to cross between parts.
All inputs are finite; a program needn't handle non-finite values.
Results may differ from a plain program's by a relative error of at most 0.0056.
Values may be sent and summed in bfloat16 or wider, within the bound.
A program may use at most 128 MiB of HBM per device.

v0:
```python
import jax
import jax.numpy as jnp
from jax import lax
from jax.sharding import PartitionSpec as P

LATENT = 16
PATCH = 2
PDIM = 64


def with_halo(cells, sides, width):
    for axis, dim in sides:
        count = lax.axis_size(axis)
        ends = count - 1
        head = lax.slice_in_dim(cells, 0, width, axis=dim)
        tail = lax.slice_in_dim(cells, cells.shape[dim] - width, cells.shape[dim], axis=dim)
        cells = jnp.concatenate(
            [
                lax.ppermute(tail, axis, [(i, (i + 1) % count) for i in range(ends)]),
                cells,
                lax.ppermute(head, axis, [((i + 1) % count, i) for i in range(ends)]),
            ],
            axis=dim,
        )
    return cells


def passed_along(block, axis, distance):
    devices = range(lax.axis_size(axis))
    route = [(i - distance, i) for i in devices if i - distance in devices]
    return lax.ppermute(block, axis, route)


def norm_silu(values):
    scaled = values * lax.rsqrt(jnp.mean(values * values, axis=-1, keepdims=True) + 1e-06)
    return jax.nn.silu(scaled)


def per_device(
    features,
    spatial_weight,
    temporal_weight,
    head_weight,
    embed_weight,
    ada_scale,
    ada_shift,
    qkv_weight,
):
    frames_dev, rows_dev, columns, channels = features.shape
    activated = norm_silu(features.astype(jnp.float32)).astype(jnp.bfloat16)
    rimmed = with_halo(activated, (("rows", 1),), 1)
    padded = jnp.pad(rimmed, ((0, 0), (0, 0), (1, 1), (0, 0)))
    spatial = jnp.zeros((frames_dev * rows_dev * columns, channels), jnp.float32)
    for tap_row in range(3):
        for tap_col in range(3):
            window = padded[:, tap_row : tap_row + rows_dev, tap_col : tap_col + columns].reshape(
                -1, channels
            )
            spatial = spatial + jnp.dot(
                window, spatial_weight[tap_row, tap_col], preferred_element_type=jnp.float32
            )
    mixed_act = (
        norm_silu(spatial).astype(jnp.bfloat16).reshape(frames_dev, rows_dev, columns, channels)
    )
    before = passed_along(mixed_act, "tm", 1)
    stacked = jnp.concatenate([before, mixed_act], axis=0)
    temporal = jnp.zeros((frames_dev * rows_dev * columns, channels), jnp.float32)
    for tap in range(3):
        temporal = temporal + jnp.dot(
            stacked[tap : tap + frames_dev].reshape(-1, channels),
            temporal_weight[tap],
            preferred_element_type=jnp.float32,
        )
    summed = features.astype(jnp.float32).reshape(-1, channels) + temporal
    latent = jnp.dot(
        norm_silu(summed).astype(jnp.bfloat16), head_weight, preferred_element_type=jnp.float32
    ).astype(jnp.bfloat16)
    latent = latent.reshape(frames_dev, 1, PATCH, columns // PATCH, PATCH, LATENT)
    patches = jnp.transpose(latent, (0, 1, 3, 2, 4, 5)).reshape(
        frames_dev, 1, columns // PATCH, PDIM
    )
    token_block = lax.all_gather(patches, "rows", axis=1, tiled=True)
    block_rows = token_block.shape[0] * token_block.shape[1] * token_block.shape[2]
    embedded = jnp.dot(
        token_block.reshape(block_rows, PDIM), embed_weight, preferred_element_type=jnp.float32
    ).astype(jnp.bfloat16)
    widened = lax.optimization_barrier(embedded).astype(jnp.float32)
    centered = widened - jnp.mean(widened, axis=-1, keepdims=True)
    spread = jnp.mean(centered * centered, axis=-1, keepdims=True)
    modulated = centered * lax.rsqrt(spread + 1e-06) * (
        1.0 + ada_scale.astype(jnp.float32)
    ) + ada_shift.astype(jnp.float32)
    normalized = modulated.astype(jnp.bfloat16)
    whole_columns = lax.all_gather(qkv_weight, "tm", axis=0, tiled=True)
    projected = jnp.dot(normalized, whole_columns, preferred_element_type=jnp.float32)
    return projected


def solution(mesh):
    return jax.shard_map(
        per_device,
        mesh=mesh,
        in_specs=(
            P(("groups", "tm"), "rows", None, None),
            P(),
            P(),
            P(),
            P(),
            P(),
            P(),
            P("tm", "rows"),
        ),
        out_specs=P(("groups", "tm"), "rows"),
        check_vma=False,
    )
```

profile of v0, /device:TPU:7, one launch (start us, length us, event | category | flops | bytes accessed | tf_op | source)
XLA Modules:
  0.0 185.0 jit_solution(10699574002116954827)
XLA Ops:
  6.6 0.7 all-gather.2.cloned.1.call-update
  7.3 0.3 copy-done.2
  7.8 0.3 multiply_convert_fusion.2
  8.1 3.2 %collective-permute-start = (bf16[2,1,96,512]{3,2,1,0:T(8,128)(2,1)S(1)}, bf16[2,1,96,512]{3,2,1,0:T(8,128)(2,1)S(1)}, u32[]{:S(2)}, u32[]{:S(2)}) collective-permute-start(bf16[2,1,96,512]{3,2,1,0:T(8,128)(2,1)S(1)} %get-tuple-element.13), channel_id=1, source_target_pairs={{0,1},{1,2},{2,3},{4,5},{5,6},{6,7},{8,9},{9,10},{10,11},{12,13},{... | collective-permute-start | bytes 589832 | tf_op jit(solution)/shard_map/ppermute | solution.py:19
  11.3 1.3 collective-permute-start.1
  12.7 2.2 %collective-permute-done = bf16[2,1,96,512]{3,2,1,0:T(8,128)(2,1)S(1)} collective-permute-done((bf16[2,1,96,512]{3,2,1,0:T(8,128)(2,1)S(1)}, bf16[2,1,96,512]{3,2,1,0:T(8,128)(2,1)S(1)}, u32[]{:S(2)}, u32[]{:S(2)}) %collective-permute-start) | collective-permute-done | bytes 196640 | tf_op jit(solution)/shard_map/ppermute | solution.py:19
  14.9 3.8 %collective-permute-done.1 = bf16[2,1,96,512]{3,2,1,0:T(8,128)(2,1)S(1)} collective-permute-done((bf16[2,1,96,512]{3,2,1,0:T(8,128)(2,1)S(1)}, bf16[2,1,96,512]{3,2,1,0:T(8,128)(2,1)S(1)}, u32[]{:S(2)}, u32[]{:S(2)}) %collective-permute-start.1) | collective-permute-done | bytes 196640 | tf_op jit(solution)/shard_map/ppermute | solution.py:21
  18.8 0.2 fusion.20
  19.0 0.3 fusion.50
  19.4 0.4 fusion.35
  19.8 0.4 fusion.26
  20.1 0.4 convolution_add_fusion.7
  20.5 0.4 convolution_add_fusion.6
  20.9 0.4 convolution_add_fusion.5
  21.3 0.4 convolution_add_fusion.4
  21.7 0.4 convolution_add_fusion.3
  22.0 0.4 convolution_add_fusion.2
  22.4 0.5 multiply_reduce_fusion.1
  22.9 0.3 multiply_convert_fusion.1
  23.2 1.3 collective-permute-start.2
  24.5 0.4 fusion.21
  24.9 3.8 %collective-permute-done.2 = bf16[2,2,96,512]{3,2,1,0:T(8,128)(2,1)S(1)} collective-permute-done((bf16[2,2,96,512]{3,2,1,0:T(8,128)(2,1)S(1)}, bf16[2,2,96,512]{3,2,1,0:T(8,128)(2,1)S(1)}, u32[]{:S(2)}, u32[]{:S(2)}) %collective-permute-start.2) | collective-permute-done | bytes 393248 | tf_op jit(solution)/shard_map/ppermute | solution.py:31
  28.7 0.4 fusion.23
  29.1 0.5 multiply_reduce_fusion
  29.6 0.4 convolution_convert_fusion.1
  30.4 10.7 %all_gather.6 = bf16[2,4,48,64]{3,2,0,1:T(8,128)(2,1)S(1)} all-gather(bf16[2,1,48,64]{3,2,0,1:T(8,128)(2,1)S(1)} %copy.16), channel_id=1, replica_groups=mesh['groups'=2,'tm'=4,'rows'=4] {'rows'}, dimensions={1}, use_global_device_ids=true | all-gather | bytes 61440 | tf_op jit(solution)/shard_map/all_gather | solution.py:82
  41.4 1.2 convolution_convert_fusion
  42.7 0.6 convert_reduce_fusion
  43.3 1.4 copy-done.1
  44.6 1.2 fusion.2
  45.8 114.1 %all-gather.2.cloned.1.call-done = bf16[5120,2304]{1,0:T(8,128)(2,1)} async-done(((bf16[1280,2304]{1,0:T(8,128)(2,1)}), bf16[5120,2304]{1,0:T(8,128)(2,1)}) %all-gather.2.cloned.1.call-update) | async-done | bytes 23592976 | tf_op jit(solution)/shard_map/all_gather | solution.py:94
  159.9 18.2 %fusion.6 = f32[384,2304]{1,0:T(8,128)} fusion(bf16[5120,2304]{1,0:T(8,128)(2,1)} %all-gather.2.cloned.1.call-done, bf16[384,5120]{1,0:T(8,128)(2,1)} %copy-done.1, f32[5120]{0:T(1024)S(1)} %convert_element_type.41, f32[5120]{0:T(1024)S(1)} %convert_add_fusion, f32[384]{0:T(512)S(1)} %add_rsqrt_fusion, f32[384]{0:T(512)S(1)} %broadcast_multiply_fusion), kind=kOutput, calls=%fused_computation.9 | convolution fusion | flops 9071493120 | bytes 31108096 | tf_op jit(solution)/shard_map/dot_general | solution.py:95
  (34 shorter events, 1.0 us)
Async XLA Ops:
  6.5 34.9 %copy-start = (bf16[64,5120]{1,0:T(8,128)(2,1)S(1)}, bf16[64,5120]{1,0:T(8,128)(2,1)}, u32[]{:S(2)}) copy-start(bf16[64,5120]{1,0:T(8,128)(2,1)} %param.12) | copy-start | bytes 1966084
  6.5 1.1 copy-start.2
  6.5 6.1 %copy-start.4 = (bf16[5120]{0:T(1024)(128)(2,1)S(1)}, bf16[5120]{0:T(1024)(128)(2,1)}, u32[]{:S(2)}) copy-start(bf16[5120]{0:T(1024)(128)(2,1)} %param.14) | copy-start | bytes 30724
  6.5 153.4 %all-gather.2.cloned.1.call-start = ((), (), s32[]{:S(2)}) async-start(), calls=%async_computation | async-start | bytes 29491200 | tf_op jit(solution)/shard_map/all_gather | solution.py:94
  6.5 12.8 %slice-start = ((s8[4718592]{0:T(1024)(128)(4,1)}), s8[524288]{0:T(1024)(128)(4,1)S(1)}, s32[]{:S(2)}) async-start(s8[4718592]{0:T(1024)(128)(4,1)} %bitcast.77), calls=%async_computation.1 | async-start | bytes 1048576
  8.1 6.8 %collective-permute-start = (bf16[2,1,96,512]{3,2,1,0:T(8,128)(2,1)S(1)}, bf16[2,1,96,512]{3,2,1,0:T(8,128)(2,1)S(1)}, u32[]{:S(2)}, u32[]{:S(2)}) collective-permute-start(bf16[2,1,96,512]{3,2,1,0:T(8,128)(2,1)S(1)} %get-tuple-element.13), channel_id=1, source_target_pairs={{0,1},{1,2},{2,3},{4,5},{5,6},{6,7},{8,9},{9,10},{10,11},{12,13},{... | collective-permute-start | bytes 589832 | tf_op jit(solution)/shard_map/ppermute | solution.py:19
  11.3 7.4 %collective-permute-start.1 = (bf16[2,1,96,512]{3,2,1,0:T(8,128)(2,1)S(1)}, bf16[2,1,96,512]{3,2,1,0:T(8,128)(2,1)S(1)}, u32[]{:S(2)}, u32[]{:S(2)}) collective-permute-start(bf16[2,1,96,512]{3,2,1,0:T(8,128)(2,1)S(1)} %get-tuple-element.14), channel_id=1, source_target_pairs={{1,0},{2,1},{3,2},{5,4},{6,5},{7,6},{9,8},{10,9},{11,10},{13,12},{... | collective-permute-start | bytes 589832 | tf_op jit(solution)/shard_map/ppermute | solution.py:21
  12.7 6.7 %slice-start.1 = ((s8[4718592]{0:T(1024)(128)(4,1)}), s8[4194304]{0:T(1024)(128)(4,1)S(1)}, s32[]{:S(2)}) async-start(s8[4718592]{0:T(1024)(128)(4,1)} %bitcast.77), calls=%async_computation.2 | async-start | bytes 8388608
  21.6 2.8 %copy-start.5 = (bf16[5120]{0:T(1024)(128)(2,1)S(1)}, bf16[5120]{0:T(1024)(128)(2,1)}, u32[]{:S(2)}) copy-start(bf16[5120]{0:T(1024)(128)(2,1)} %param.13) | copy-start | bytes 30724
  21.6 2.9 %copy-start.3 = (bf16[3,512,512]{2,1,0:T(8,128)(2,1)S(1)}, bf16[3,512,512]{2,1,0:T(8,128)(2,1)}, u32[]{:S(2)}) copy-start(bf16[3,512,512]{2,1,0:T(8,128)(2,1)} %param.10) | copy-start | bytes 4718596
  22.9 6.7 %copy-start.6 = (bf16[512,16]{0,1:T(8,128)(2,1)S(1)}, bf16[512,16]{0,1:T(8,128)(2,1)}, u32[]{:S(2)}) copy-start(bf16[512,16]{0,1:T(8,128)(2,1)} %param.11) | copy-start | bytes 49156
  23.2 5.5 %collective-permute-start.2 = (bf16[2,2,96,512]{3,2,1,0:T(8,128)(2,1)S(1)}, bf16[2,2,96,512]{3,2,1,0:T(8,128)(2,1)S(1)}, u32[]{:S(2)}, u32[]{:S(2)}) collective-permute-start(bf16[2,2,96,512]{3,2,1,0:T(8,128)(2,1)S(1)} %bitcast.80), channel_id=1, source_target_pairs={{0,4},{4,8},{8,12},{1,5},{5,9},{9,13},{2,6},{6,10},{10,14},{3,7},{... | collective-permute-start | bytes 1179656 | tf_op jit(solution)/shard_map/ppermute | solution.py:31
  42.7 2.0 %copy-start.1 = (bf16[384,5120]{1,0:T(8,128)(2,1)}, bf16[384,5120]{1,0:T(8,128)(2,1)S(1)}, u32[]{:S(2)}) copy-start(bf16[384,5120]{1,0:T(8,128)(2,1)S(1)} %convolution_convert_fusion) | copy-start | bytes 11796484
Sparse Core Ops, SparseCore 0:
  8.9 150.9 all-gather.1
where the time goes:
time: 185 us
  waiting for transfers between devices  125 us (68%)
  matrix products  24.4 us (13%)
  between operations  13.7 us (7%)
  blocking collectives  10.7 us (6%)
  starting transfers between devices  5.8 us (3%)
  other arithmetic  2.89 us (2%)
  local copies, waits for them, and re-layouts  2.73 us (1%)
    all_gather x1, waiting for transfers between devices, per_device(): whole_columns = lax.all_gather(qkv_weight, 'tm', axis=0, tiled=True)  114 us
    dot_general x1, matrix products, per_device(): jnp.dot(normalized, whole_columns, preferred_element_type=jnp.float32)  18.2 us
    all_gather x1, blocking collectives, per_device(): token_block = lax.all_gather(patches, 'rows', axis=1, tiled=True)  10.7 us
    ppermute x1, waiting for transfers between devices, with_halo(): lax.ppermute(head, axis, [((i + 1) % count, i) for i in range(ends)])  3.84 us
    ppermute x1, waiting for transfers between devices, passed_along(): return lax.ppermute(block, axis, route)  3.8 us
  transfers between devices with their start and end apart: 4, of which 4 were waited for; matrix products, arithmetic and copies ran while one was open for 5% of the time, Pallas kernels for 0%

commit v1 on v0

--- a/solution.py
+++ b/solution.py
@@ -91,7 +91,9 @@
         1.0 + ada_scale.astype(jnp.float32)
     ) + ada_shift.astype(jnp.float32)
     normalized = modulated.astype(jnp.bfloat16)
-    whole_columns = lax.all_gather(qkv_weight, "tm", axis=0, tiled=True)
+    whole_columns = jnp.concatenate(
+        lax.all_to_all(jnp.stack([qkv_weight] * lax.axis_size("tm")), "tm", 0, 0), axis=0
+    )
     projected = jnp.dot(normalized, whole_columns, preferred_element_type=jnp.float32)
     return projected
 

time: 185 us -> 316 us (1.71)
  the two profiles are of different devices: /device:TPU:7 before, /device:TPU:4 now
where the time goes in v1:
time: 316 us
  waiting for transfers between devices  243 us (77%)
  matrix products  25.4 us (8%)
  starting transfers between devices  16 us (5%)
  blocking collectives  15.2 us (5%)
  local copies, waits for them, and re-layouts  12.5 us (4%)
    ppermute x1, waiting for transfers between devices, passed_along(): return lax.ppermute(block, axis, route)  239 us
    dot_general x1, matrix products, per_device(): jnp.dot(normalized, whole_columns, preferred_element_type=jnp.float32)  18.1 us
    all_gather x1, blocking collectives, per_device(): token_block = lax.all_gather(patches, 'rows', axis=1, tiled=True)  15.2 us
    another operation x1, local copies, waits for them, and re-layouts, per_device(): jnp.stack([qkv_weight] * lax.axis_size('tm'))  10.2 us
    all_to_all x1, starting transfers between devices, per_device(): lax.all_to_all(jnp.stack([qkv_weight] * lax.axis_size('tm')), 'tm', 0, 0)  8.26 us
  transfers between devices with their start and end apart: 4, of which 3 were waited for; matrix products, arithmetic and copies ran while one was open for 4% of the time, Pallas kernels for 0%

profile of v1, /device:TPU:4, one launch (start us, length us, event | category | flops | bytes accessed | tf_op | source)
XLA Modules:
  0.0 315.7 jit_solution(8195053898487390686)
XLA Ops:
  0.0 10.2 %stack.2 = bf16[4,1280,2304]{2,1,0:T(8,128)(2,1)} broadcast(bf16[1280,2304]{1,0:T(8,128)(2,1)} %param.15), dimensions={1,2} | broadcast | bytes 29491200 | tf_op jit(solution)/shard_map/stack | solution.py:95
  10.2 8.3 %all-to-all-start = ((bf16[4,1280,2304]{2,1,0:T(8,128)(2,1)}), bf16[4,1280,2304]{2,1,0:T(8,128)(2,1)}, u32[]{:S(2)}, u32[]{:S(2)}) async-start(bf16[4,1280,2304]{2,1,0:T(8,128)(2,1)} %stack.2), calls=%async_computation | async-start | bytes 47185920 | tf_op jit(solution)/shard_map/all_to_all | solution.py:95
  18.5 0.2 multiply_reduce_fusion.2
  18.6 0.3 multiply_convert_fusion.2
  19.0 1.3 collective-permute-start.1
  20.3 4.6 %collective-permute-start = (bf16[2,1,96,512]{3,2,1,0:T(8,128)(2,1)S(1)}, bf16[2,1,96,512]{3,2,1,0:T(8,128)(2,1)S(1)}, u32[]{:S(2)}, u32[]{:S(2)}) collective-permute-start(bf16[2,1,96,512]{3,2,1,0:T(8,128)(2,1)S(1)} %get-tuple-element.13), channel_id=1, source_target_pairs={{0,1},{1,2},{2,3},{4,5},{5,6},{6,7},{8,9},{9,10},{10,11},{12,13},{... | collective-permute-start | bytes 589832 | tf_op jit(solution)/shard_map/ppermute | solution.py:19
  24.9 3.2 %collective-permute-done.1 = bf16[2,1,96,512]{3,2,1,0:T(8,128)(2,1)S(1)} collective-permute-done((bf16[2,1,96,512]{3,2,1,0:T(8,128)(2,1)S(1)}, bf16[2,1,96,512]{3,2,1,0:T(8,128)(2,1)S(1)}, u32[]{:S(2)}, u32[]{:S(2)}) %collective-permute-start.1) | collective-permute-done | bytes 196640 | tf_op jit(solution)/shard_map/ppermute | solution.py:21
  28.1 1.2 collective-permute-done
  29.4 0.2 fusion.20
  29.6 0.3 fusion.50
  29.9 1.4 fusion.26
  31.3 0.4 fusion.35
  31.7 0.4 convolution_add_fusion.7
  32.1 0.4 convolution_add_fusion.6
  32.5 0.4 convolution_add_fusion.5
  32.8 0.4 convolution_add_fusion.4
  33.2 0.4 convolution_add_fusion.3
  33.6 0.4 convolution_add_fusion.2
  34.0 0.5 multiply_reduce_fusion.1
  34.5 0.3 multiply_convert_fusion.1
  34.7 1.9 collective-permute-start.2
  36.7 0.4 fusion.21
  37.1 239.0 %collective-permute-done.2 = bf16[2,2,96,512]{3,2,1,0:T(8,128)(2,1)S(1)} collective-permute-done((bf16[2,2,96,512]{3,2,1,0:T(8,128)(2,1)S(1)}, bf16[2,2,96,512]{3,2,1,0:T(8,128)(2,1)S(1)}, u32[]{:S(2)}, u32[]{:S(2)}) %collective-permute-start.2) | collective-permute-done | bytes 393248 | tf_op jit(solution)/shard_map/ppermute | solution.py:31
  276.1 0.4 fusion.23
  276.5 0.5 multiply_reduce_fusion
  277.0 0.4 convolution_convert_fusion.1
  277.8 15.2 %all_gather.3 = bf16[2,4,48,64]{3,2,0,1:T(8,128)(2,1)S(1)} all-gather(bf16[2,1,48,64]{3,2,0,1:T(8,128)(2,1)S(1)} %copy.16), channel_id=1, replica_groups=mesh['groups'=2,'tm'=4,'rows'=4] {'rows'}, dimensions={1}, use_global_device_ids=true | all-gather | bytes 61440 | tf_op jit(solution)/shard_map/all_gather | solution.py:82
  293.3 1.2 convolution_convert_fusion
  294.5 0.6 convert_reduce_fusion
  295.1 1.3 copy-done.2
  296.4 1.2 fusion.2
  297.5 18.1 %fusion.6 = f32[384,2304]{1,0:T(8,128)} fusion(bf16[5120,2304]{1,0:T(8,128)(2,1)} %bitcast.28, bf16[384,5120]{1,0:T(8,128)(2,1)} %copy-done.2, f32[5120]{0:T(1024)S(1)} %convert_element_type.41, f32[5120]{0:T(1024)S(1)} %convert_add_fusion, f32[384]{0:T(512)S(1)} %add_rsqrt_fusion, f32[384]{0:T(512)S(1)} %broadcast_multiply_fusion), kind=kOutput, calls=%fused_computation.9 | convolution fusion | flops 9071493120 | bytes 31108096 | tf_op jit(solution)/shard_map/dot_general | solution.py:97
  (33 shorter events, 0.9 us)
Async XLA Ops:
  0.0 293.2 %copy-start = (bf16[64,5120]{1,0:T(8,128)(2,1)S(1)}, bf16[64,5120]{1,0:T(8,128)(2,1)}, u32[]{:S(2)}) copy-start(bf16[64,5120]{1,0:T(8,128)(2,1)} %param.12) | copy-start | bytes 1966084
  10.2 8.3 %copy-start.4 = (bf16[2,2,96,512]{3,2,1,0:T(8,128)(2,1)S(1)}, bf16[2,2,96,512]{3,2,1,0:T(8,128)(2,1)}, u32[]{:S(2)}) copy-start(bf16[2,2,96,512]{3,2,1,0:T(8,128)(2,1)} %param.8) | copy-start | bytes 1179652
  10.2 14.7 %copy-start.6 = (bf16[5120]{0:T(1024)(128)(2,1)S(1)}, bf16[5120]{0:T(1024)(128)(2,1)}, u32[]{:S(2)}) copy-start(bf16[5120]{0:T(1024)(128)(2,1)} %param.14) | copy-start | bytes 30724
  10.2 287.3 %all-to-all-start = ((bf16[4,1280,2304]{2,1,0:T(8,128)(2,1)}), bf16[4,1280,2304]{2,1,0:T(8,128)(2,1)}, u32[]{:S(2)}, u32[]{:S(2)}) async-start(bf16[4,1280,2304]{2,1,0:T(8,128)(2,1)} %stack.2), calls=%async_computation | async-start | bytes 47185920 | tf_op jit(solution)/shard_map/all_to_all | solution.py:95
  19.0 9.1 %collective-permute-start.1 = (bf16[2,1,96,512]{3,2,1,0:T(8,128)(2,1)S(1)}, bf16[2,1,96,512]{3,2,1,0:T(8,128)(2,1)S(1)}, u32[]{:S(2)}, u32[]{:S(2)}) collective-permute-start(bf16[2,1,96,512]{3,2,1,0:T(8,128)(2,1)S(1)} %get-tuple-element.14), channel_id=1, source_target_pairs={{1,0},{2,1},{3,2},{5,4},{6,5},{7,6},{9,8},{10,9},{11,10},{13,12},{... | collective-permute-start | bytes 589832 | tf_op jit(solution)/shard_map/ppermute | solution.py:21
  20.3 9.0 %collective-permute-start = (bf16[2,1,96,512]{3,2,1,0:T(8,128)(2,1)S(1)}, bf16[2,1,96,512]{3,2,1,0:T(8,128)(2,1)S(1)}, u32[]{:S(2)}, u32[]{:S(2)}) collective-permute-start(bf16[2,1,96,512]{3,2,1,0:T(8,128)(2,1)S(1)} %get-tuple-element.13), channel_id=1, source_target_pairs={{0,1},{1,2},{2,3},{4,5},{5,6},{6,7},{8,9},{9,10},{10,11},{12,13},{... | collective-permute-start | bytes 589832 | tf_op jit(solution)/shard_map/ppermute | solution.py:19
  24.9 6.4 %copy-start.3 = (bf16[3,3,512,512]{3,2,1,0:T(8,128)(2,1)S(1)}, bf16[3,3,512,512]{3,2,1,0:T(8,128)(2,1)}, u32[]{:S(2)}) copy-start(bf16[3,3,512,512]{3,2,1,0:T(8,128)(2,1)} %param.9) | copy-start | bytes 14155780
  33.2 3.5 %copy-start.7 = (bf16[5120]{0:T(1024)(128)(2,1)S(1)}, bf16[5120]{0:T(1024)(128)(2,1)}, u32[]{:S(2)}) copy-start(bf16[5120]{0:T(1024)(128)(2,1)} %param.13) | copy-start | bytes 30724
  33.2 3.5 %copy-start.5 = (bf16[3,512,512]{2,1,0:T(8,128)(2,1)S(1)}, bf16[3,512,512]{2,1,0:T(8,128)(2,1)}, u32[]{:S(2)}) copy-start(bf16[3,512,512]{2,1,0:T(8,128)(2,1)} %param.10) | copy-start | bytes 4718596
  34.4 242.6 %copy-start.8 = (bf16[512,16]{0,1:T(8,128)(2,1)S(1)}, bf16[512,16]{0,1:T(8,128)(2,1)}, u32[]{:S(2)}) copy-start(bf16[512,16]{0,1:T(8,128)(2,1)} %param.11) | copy-start | bytes 49156
  34.7 241.3 %collective-permute-start.2 = (bf16[2,2,96,512]{3,2,1,0:T(8,128)(2,1)S(1)}, bf16[2,2,96,512]{3,2,1,0:T(8,128)(2,1)S(1)}, u32[]{:S(2)}, u32[]{:S(2)}) collective-permute-start(bf16[2,2,96,512]{3,2,1,0:T(8,128)(2,1)S(1)} %bitcast.79), channel_id=1, source_target_pairs={{0,4},{4,8},{8,12},{1,5},{5,9},{9,13},{2,6},{6,10},{10,14},{3,7},{... | collective-permute-start | bytes 1179656 | tf_op jit(solution)/shard_map/ppermute | solution.py:31
  294.5 1.9 copy-start.2
  297.5 18.1 %copy-start.1 = (bf16[64,5120]{1,0:T(8,128)(2,1)S(1)}, bf16[64,5120]{1,0:T(8,128)(2,1)}, u32[]{:S(2)}) copy-start(bf16[64,5120]{1,0:T(8,128)(2,1)} %param.12) | copy-start | bytes 1966084
